TPU v7x, 32 devices: a whole 2x2x4 slice. The times are simulated.
32 devices in a mesh: blk: 16 (over z, y, core), tile: 2 (over x).
Axes of the slice: x: 2, y: 2, z: 4, core: 2. Of those that a mesh axis runs over, the one named last changes fastest.
Arguments:
- positions: float32 [3, 2048], P(None, ('blk', 'tile')), as said below
- noise_vectors: float32 [3, 32, 2048], P(None, None, ('blk', 'tile')), may hold values from -6 to 6
- spectrum_bounds: float32 [2], replicated, as said below
Outputs:
- displacement: float32 [3, 32, 2048], P(None, None, ('blk', 'tile'))
- images: float32 [2, 3, 32, 2048], P(None, None, None, ('blk', 'tile'))
Inputs may be any that keep to these rules, and one draw needn't show every extreme that they name: `positions`: coordinates lie in a cube whose edge is the cube root of 41.9 * 2048; particle n's third coordinate lies between n and n + 1 times that edge divided by 2048. `spectrum_bounds`: the first entry lies between 0.15 and 0.35; the second exceeds 50 times the first.
All inputs are finite; a program needn't handle non-finite values.
Results may differ from a plain program's by a relative error of at most 0.0003.
Values sent between devices are 32-bit elements; how exact they have to be, the bound alone decides.
No kernel may reach another device: no remote copies, remote signals or barrier semaphores. Data moves between devices by JAX's collectives and lax.ppermute only.
A program may use at most 64 MiB of HBM per device.

v0:
```python
import math
import jax
import jax.numpy as jnp
from jax import lax
from jax.sharding import PartitionSpec as P

soft_core = 1e-06
node_count = 32


def from_partner(block, axis, apart):
    count = lax.axis_size(axis)
    route = []
    for low in range(count):
        high = low | 1 << apart
        if high != low and high < count:
            route += [(low, high), (high, low)]
    return lax.ppermute(block, axis, route)


def kernel(targets, sources):
    offset = targets[:, :, None] - sources[:, None, :]
    squared = jnp.sum(offset * offset, axis=0) + soft_core
    distance = jnp.sqrt(squared)
    inverse = 1.0 / distance
    cubed = inverse * inverse * inverse
    intersection = distance < 2.0
    scalar_part = jnp.where(intersection, 1.0 - 0.28125 * distance, 0.75 * inverse + 0.5 * cubed)
    dyadic_part = jnp.where(
        intersection, 0.09375 * inverse, 0.75 * cubed - 1.5 * cubed * inverse * inverse
    )
    identity = jnp.eye(3, dtype=targets.dtype)
    return (
        identity[:, :, None, None] * scalar_part[None, None]
        + dyadic_part[None, None] * offset[:, None] * offset[None, :]
    )


def contract(tensor, vectors):
    return jnp.einsum("abij,bkj->aki", tensor, vectors, precision=lax.Precision.HIGHEST)


def weights_from(bounds):
    lowest = bounds[0]
    highest = bounds[1]
    center = 0.5 * (highest + lowest)
    spread = 0.5 * (highest - lowest)
    angles = math.pi * (jnp.arange(node_count, dtype=bounds.dtype) + 0.5) / node_count
    samples = jnp.sqrt(center + spread * jnp.cos(angles))
    weights = [2.0 / node_count * jnp.sum(samples * jnp.cos(order * angles)) for order in range(3)]
    return (center, spread, weights)


def apply_blocks(targets, incoming):
    return contract(kernel(targets, incoming[:, 0, :]), incoming[:, 1:, :])


def grid_product(packed, positions):
    half_bits = (lax.axis_size("blk").bit_length() - 1) // 2
    block_number = lax.axis_index("blk")
    sources = lax.all_gather(packed, "tile", axis=2, tiled=True)
    for bit_number in range(half_bits, 2 * half_bits):
        partner = from_partner(sources, "blk", bit_number)
        sources = jnp.concatenate([sources, partner], axis=2)
    targets = positions
    for bit_number in range(half_bits):
        partner = from_partner(targets, "blk", bit_number)
        own_bit = block_number // (1 << bit_number) % 2
        targets = jnp.where(
            own_bit == 1,
            jnp.concatenate([partner, targets], axis=1),
            jnp.concatenate([targets, partner], axis=1),
        )
    partial_value = apply_blocks(targets, sources)
    for bit_number in reversed(range(half_bits)):
        half_width = partial_value.shape[2] // 2
        own_bit = block_number // (1 << bit_number) % 2
        kept_half = lax.dynamic_slice_in_dim(partial_value, own_bit * half_width, half_width, 2)
        sent_half = lax.dynamic_slice_in_dim(
            partial_value, (1 - own_bit) * half_width, half_width, 2
        )
        partial_value = kept_half + from_partner(sent_half, "blk", bit_number)
    return partial_value


def mobility(vectors, positions):
    packed = jnp.concatenate([positions[:, None, :], vectors], axis=1)
    return grid_product(packed, positions)


def body(positions, noise_vectors, spectrum_bounds):
    center, spread, weights = weights_from(spectrum_bounds)
    first_image = mobility(noise_vectors, positions)
    linear_term = (first_image - center * noise_vectors) / spread
    second_image = mobility(linear_term, positions)
    quadratic_term = 2.0 * (second_image - center * linear_term) / spread - noise_vectors
    displacement = (
        0.5 * weights[0] * noise_vectors + weights[1] * linear_term + weights[2] * quadratic_term
    )
    return (displacement, jnp.stack([first_image, second_image]))


def solution(mesh):
    return jax.shard_map(
        body,
        mesh=mesh,
        in_specs=(P(None, ("blk", "tile")), P(None, None, ("blk", "tile")), P()),
        out_specs=(P(None, None, ("blk", "tile")), P(None, None, None, ("blk", "tile"))),
        check_vma=False,
    )
```

profile of v0, /device:TPU:1, one launch (start us, length us, event | category | flops | bytes accessed | tf_op | source)
XLA Modules:
  0.0 68.6 jit_solution(18296448946351239026)
XLA Ops:
  0.7 0.7 broadcast_in_dim.2
  1.4 0.8 %pad_maximum_fusion.6 = f32[3,33,64]{2,1,0:T(8,128)S(1)} fusion(f32[3,1,64]{2,1,0:T(1,128)S(1)} %broadcast_in_dim.2, f32[3,32,64]{2,1,0:T(8,128)} %param.4), kind=kLoop, calls=%fused_computation.52 | loop fusion | flops 6336 | bytes 50688 | tf_op jit(solution)/shard_map/concatenate | solution.py:87
  2.3 7.2 %all_gather.6 = f32[3,33,128]{1,0,2:T(4,128)S(1)} all-gather(f32[3,33,64]{1,0,2:T(4,128)S(1)} %copy.14), channel_id=1, replica_groups=mesh['blk'=16,'tile'=2] {'tile'}, dimensions={2}, use_global_device_ids=true | all-gather | bytes 76032 | tf_op jit(solution)/shard_map/all_gather | solution.py:61
  9.6 1.3 %collective-permute-start = (f32[3,33,128]{2,1,0:T(8,128)S(1)}, f32[3,33,128]{2,1,0:T(8,128)S(1)}, u32[]{:S(2)}, u32[]{:S(2)}) collective-permute-start(f32[3,33,128]{2,1,0:T(8,128)S(1)} %copy.17), channel_id=1, source_target_pairs={{0,8},{8,0},{2,10},{10,2},{4,12},{12,4},{6,14},{14,6},{16,24},{24,... | collective-permute-start | bytes 152072 | tf_op jit(solution)/shard_map/ppermute | solution.py:18
  11.0 0.8 %maximum_select_fusion.1 = f32[3,128]{1,0:T(4,128)S(1)} fusion(f32[3,64]{1,0:T(4,128)} %param.3, f32[3,64]{1,0:T(4,128)S(1)} %collective-permute-done.2, pred[]{:T(512)S(6)} %eq.29), kind=kLoop, calls=%fused_computation.68 | loop fusion | flops 1152 | bytes 3073 | tf_op jit(solution)/shard_map/jit(_where)/select_n | solution.py:69
  11.8 1.2 %collective-permute-start.3 = (f32[3,128]{1,0:T(4,128)S(1)}, f32[3,128]{1,0:T(4,128)S(1)}, u32[]{:S(2)}, u32[]{:S(2)}) collective-permute-start(f32[3,128]{1,0:T(4,128)S(1)} %maximum_select_fusion.1), channel_id=1, source_target_pairs={{0,4},{4,0},{2,6},{6,2},{8,12},{12,8},{10,14},{14,10},{16,20},{20,... | collective-permute-start | bytes 4616 | tf_op jit(solution)/shard_map/ppermute | solution.py:18
  13.1 2.4 %collective-permute-start.1 = (f32[3,33,256]{2,1,0:T(8,128)S(1)}, f32[3,33,256]{2,1,0:T(8,128)S(1)}, u32[]{:S(2)}, u32[]{:S(2)}) collective-permute-start(f32[3,33,256]{2,1,0:T(8,128)S(1)} %pad_maximum_fusion.2), channel_id=1, source_target_pairs={{0,16},{16,0},{2,18},{18,2},{4,20},{20,4},{6,22},{22,6},{8,24},{24... | collective-permute-start | bytes 304136 | tf_op jit(solution)/shard_map/ppermute | solution.py:18
  15.5 4.4 %collective-permute-done.1 = f32[3,33,256]{2,1,0:T(8,128)S(1)} collective-permute-done((f32[3,33,256]{2,1,0:T(8,128)S(1)}, f32[3,33,256]{2,1,0:T(8,128)S(1)}, u32[]{:S(2)}, u32[]{:S(2)}) %collective-permute-start.1) | collective-permute-done | bytes 101408 | tf_op jit(solution)/shard_map/ppermute | solution.py:18
  20.9 4.6 %fusion.16 = f32[32,3,256]{2,0,1:T(8,128)S(1)} fusion(f32[3,256,512]{2,1,0:T(8,128)S(1)} %get-tuple-element.13, f32[3,256,512]{2,1,0:T(8,128)S(1)} %get-tuple-element.12, f32[256,512]{1,0:T(8,128)S(1)} %get-tuple-element.4, f32[3,3]{1,0:T(4,128)S(1)} %fusion.38, f32[3,33,512]{2,1,0:T(8,128)S(1)} %pad_maximum_fusion), kind=kOutput, calls=%fused_computation.20 | convolution fusion | flops 456523776 | bytes 3966976 | tf_op jit(solution)/shard_map/abij,bkj->aki/dot_general | solution.py:40
  25.5 0.6 collective-permute-start.4
  26.1 2.4 %collective-permute-done.4 = f32[3,32,128]{2,1,0:T(8,128)S(1)} collective-permute-done((f32[3,32,128]{2,1,0:T(8,128)S(1)}, f32[3,32,128]{2,1,0:T(8,128)S(1)}, u32[]{:S(2)}, u32[]{:S(2)}) %collective-permute-start.4) | collective-permute-done | bytes 49184 | tf_op jit(solution)/shard_map/ppermute | solution.py:18
  28.6 3.7 %collective-permute-start.5 = (f32[3,32,64]{2,1,0:T(8,128)S(1)}, f32[3,32,64]{2,1,0:T(8,128)S(1)}, u32[]{:S(2)}, u32[]{:S(2)}) collective-permute-start(f32[3,32,64]{2,1,0:T(8,128)S(1)} %constant_dynamic-slice_fusion.1), channel_id=1, source_target_pairs={{0,2},{2,0},{4,6},{6,4},{8,10},{10,8},{12,14},{14,12},{16,18},{18,... | collective-permute-start | bytes 73736 | tf_op jit(solution)/shard_map/ppermute | solution.py:18
  35.7 5.7 %all_gather.7 = f32[3,33,128]{1,0,2:T(4,128)S(1)} all-gather(f32[3,33,64]{1,0,2:T(4,128)S(1)} %copy.18), channel_id=1, replica_groups=mesh['blk'=16,'tile'=2] {'tile'}, dimensions={2}, use_global_device_ids=true | all-gather | bytes 76032 | tf_op jit(solution)/shard_map/all_gather | solution.py:61
  41.8 2.9 %collective-permute-done.6 = f32[3,33,128]{2,1,0:T(8,128)S(1)} collective-permute-done((f32[3,33,128]{2,1,0:T(8,128)S(1)}, f32[3,33,128]{2,1,0:T(8,128)S(1)}, u32[]{:S(2)}, u32[]{:S(2)}) %collective-permute-start.6) | collective-permute-done | bytes 50720 | tf_op jit(solution)/shard_map/ppermute | solution.py:18
  44.7 1.9 %collective-permute-start.7 = (f32[3,33,256]{2,1,0:T(8,128)S(1)}, f32[3,33,256]{2,1,0:T(8,128)S(1)}, u32[]{:S(2)}, u32[]{:S(2)}) collective-permute-start(f32[3,33,256]{2,1,0:T(8,128)S(1)} %pad_maximum_fusion.3), channel_id=1, source_target_pairs={{0,16},{16,0},{2,18},{18,2},{4,20},{20,4},{6,22},{22,6},{8,24},{24... | collective-permute-start | bytes 304136 | tf_op jit(solution)/shard_map/ppermute | solution.py:18
  46.6 4.5 %collective-permute-done.7 = f32[3,33,256]{2,1,0:T(8,128)S(1)} collective-permute-done((f32[3,33,256]{2,1,0:T(8,128)S(1)}, f32[3,33,256]{2,1,0:T(8,128)S(1)}, u32[]{:S(2)}, u32[]{:S(2)}) %collective-permute-start.7) | collective-permute-done | bytes 101408 | tf_op jit(solution)/shard_map/ppermute | solution.py:18
  52.1 4.6 %fusion.19 = f32[32,3,256]{2,0,1:T(8,128)S(1)} fusion(f32[3,256,512]{2,1,0:T(8,128)S(1)} %get-tuple-element.11, f32[3,256,512]{2,1,0:T(8,128)S(1)} %get-tuple-element.10, f32[256,512]{1,0:T(8,128)S(1)} %get-tuple-element.2, f32[3,3]{1,0:T(4,128)S(1)} %fusion.38, f32[3,33,512]{2,1,0:T(8,128)S(1)} %pad_maximum_fusion.1), kind=kOutput, calls=%fused_computation.21 | convolution fusion | flops 456523776 | bytes 3966976 | tf_op jit(solution)/shard_map/abij,bkj->aki/dot_general | solution.py:40
  56.7 1.0 %collective-permute-start.8 = (f32[3,32,128]{2,1,0:T(8,128)S(1)}, f32[3,32,128]{2,1,0:T(8,128)S(1)}, u32[]{:S(2)}, u32[]{:S(2)}) collective-permute-start(f32[3,32,128]{2,1,0:T(8,128)S(1)} %dynamic-slice_bitcast_fusion), channel_id=1, source_target_pairs={{0,4},{4,0},{2,6},{6,2},{8,12},{12,8},{10,14},{14,10},{16,20},{20,... | collective-permute-start | bytes 147464 | tf_op jit(solution)/shard_map/ppermute | solution.py:18
  57.7 2.0 %collective-permute-done.8 = f32[3,32,128]{2,1,0:T(8,128)S(1)} collective-permute-done((f32[3,32,128]{2,1,0:T(8,128)S(1)}, f32[3,32,128]{2,1,0:T(8,128)S(1)}, u32[]{:S(2)}, u32[]{:S(2)}) %collective-permute-start.8) | collective-permute-done | bytes 49184 | tf_op jit(solution)/shard_map/ppermute | solution.py:18
  59.8 4.1 %collective-permute-start.9 = (f32[3,32,64]{2,1,0:T(8,128)S(1)}, f32[3,32,64]{2,1,0:T(8,128)S(1)}, u32[]{:S(2)}, u32[]{:S(2)}) collective-permute-start(f32[3,32,64]{2,1,0:T(8,128)S(1)} %constant_dynamic-slice_fusion), channel_id=1, source_target_pairs={{0,2},{2,0},{4,6},{6,4},{8,10},{10,8},{12,14},{14,12},{16,18},{18,... | collective-permute-start | bytes 73736 | tf_op jit(solution)/shard_map/ppermute | solution.py:18
  63.8 0.7 %multiply_reduce_fusion.2 = (f32[]{:T(128)}, f32[]{:T(128)}) fusion(f32[]{:T(128)} %bitcast.1, f32[]{:T(128)} %bitcast), kind=kLoop, calls=%fused_computation.73 | loop fusion | flops 286 | bytes 16 | tf_op jit(solution)/shard_map/reduce_sum | solution.py:50
  65.9 0.7 multiply_reduce_fusion.4
  67.2 0.7 %fusion.37 = (f32[1,3,32,64]{3,2,1,0:T(8,128)S(1)}, f32[3,32,64]{2,1,0:T(8,128)}) fusion(f32[3,32,64]{2,1,0:T(8,128)S(1)} %collective-permute-done.9, f32[3,32,128]{2,1,0:T(8,128)S(1)} %bitcast_add_fusion, s32[]{:T(128)S(6)} %select_n.117, f32[3,32,64]{2,1,0:T(8,128)S(1)} %copy-done, f32[]{:T(128)} %bitcast.1, f32[3,32,64]{2,1,0:T(8,128)S(1)} %get-tuple-element.7, ...), kind=kLoop, calls=%fused_computation.62 | loop fusion | flops 67584 | bytes 147480 | tf_op jit(solution)/shard_map/stack | solution.py:100
  67.9 0.6 pad_maximum_fusion.4
  (40 shorter events, 3.6 us)
Async XLA Ops:
  0.6 10.4 %collective-permute-start.2 = (f32[3,64]{1,0:T(4,128)}, f32[3,64]{1,0:T(4,128)S(1)}, u32[]{:S(2)}, u32[]{:S(2)}) collective-permute-start(f32[3,64]{1,0:T(4,128)} %param.3), channel_id=1, source_target_pairs={{0,2},{2,0},{4,6},{6,4},{8,10},{10,8},{12,14},{14,12},{16,18},{18,... | collective-permute-start | bytes 2312 | tf_op jit(solution)/shard_map/ppermute | solution.py:18
  9.6 3.4 %collective-permute-start = (f32[3,33,128]{2,1,0:T(8,128)S(1)}, f32[3,33,128]{2,1,0:T(8,128)S(1)}, u32[]{:S(2)}, u32[]{:S(2)}) collective-permute-start(f32[3,33,128]{2,1,0:T(8,128)S(1)} %copy.17), channel_id=1, source_target_pairs={{0,8},{8,0},{2,10},{10,2},{4,12},{12,4},{6,14},{14,6},{16,24},{24,... | collective-permute-start | bytes 152072 | tf_op jit(solution)/shard_map/ppermute | solution.py:18
  11.8 3.6 %collective-permute-start.3 = (f32[3,128]{1,0:T(4,128)S(1)}, f32[3,128]{1,0:T(4,128)S(1)}, u32[]{:S(2)}, u32[]{:S(2)}) collective-permute-start(f32[3,128]{1,0:T(4,128)S(1)} %maximum_select_fusion.1), channel_id=1, source_target_pairs={{0,4},{4,0},{2,6},{6,2},{8,12},{12,8},{10,14},{14,10},{16,20},{20,... | collective-permute-start | bytes 4616 | tf_op jit(solution)/shard_map/ppermute | solution.py:18
  13.1 6.8 %collective-permute-start.1 = (f32[3,33,256]{2,1,0:T(8,128)S(1)}, f32[3,33,256]{2,1,0:T(8,128)S(1)}, u32[]{:S(2)}, u32[]{:S(2)}) collective-permute-start(f32[3,33,256]{2,1,0:T(8,128)S(1)} %pad_maximum_fusion.2), channel_id=1, source_target_pairs={{0,16},{16,0},{2,18},{18,2},{4,20},{20,4},{6,22},{22,6},{8,24},{24... | collective-permute-start | bytes 304136 | tf_op jit(solution)/shard_map/ppermute | solution.py:18
  20.9 11.4 %copy-start.1 = (f32[2]{0:T(128)S(1)}, f32[2]{0:T(128)}, u32[]{:S(2)}) copy-start(f32[2]{0:T(128)} %param.5) | copy-start | bytes 28
  20.9 14.6 %copy-start = (f32[3,32,64]{2,1,0:T(8,128)S(1)}, f32[3,32,64]{2,1,0:T(8,128)}, u32[]{:S(2)}) copy-start(f32[3,32,64]{2,1,0:T(8,128)} %param.4) | copy-start | bytes 73732
  25.5 3.0 %collective-permute-start.4 = (f32[3,32,128]{2,1,0:T(8,128)S(1)}, f32[3,32,128]{2,1,0:T(8,128)S(1)}, u32[]{:S(2)}, u32[]{:S(2)}) collective-permute-start(f32[3,32,128]{2,1,0:T(8,128)S(1)} %dynamic-slice_bitcast_fusion.1), channel_id=1, source_target_pairs={{0,4},{4,0},{2,6},{6,2},{8,12},{12,8},{10,14},{14,10},{16,20},{20,... | collective-permute-start | bytes 147464 | tf_op jit(solution)/shard_map/ppermute | solution.py:18
  28.6 6.9 %collective-permute-start.5 = (f32[3,32,64]{2,1,0:T(8,128)S(1)}, f32[3,32,64]{2,1,0:T(8,128)S(1)}, u32[]{:S(2)}, u32[]{:S(2)}) collective-permute-start(f32[3,32,64]{2,1,0:T(8,128)S(1)} %constant_dynamic-slice_fusion.1), channel_id=1, source_target_pairs={{0,2},{2,0},{4,6},{6,4},{8,10},{10,8},{12,14},{14,12},{16,18},{18,... | collective-permute-start | bytes 73736 | tf_op jit(solution)/shard_map/ppermute | solution.py:18
  41.5 3.1 %collective-permute-start.6 = (f32[3,33,128]{2,1,0:T(8,128)S(1)}, f32[3,33,128]{2,1,0:T(8,128)S(1)}, u32[]{:S(2)}, u32[]{:S(2)}) collective-permute-start(f32[3,33,128]{2,1,0:T(8,128)S(1)} %copy.21), channel_id=1, source_target_pairs={{0,8},{8,0},{2,10},{10,2},{4,12},{12,4},{6,14},{14,6},{16,24},{24,... | collective-permute-start | bytes 152072 | tf_op jit(solution)/shard_map/ppermute | solution.py:18
  44.7 6.4 %collective-permute-start.7 = (f32[3,33,256]{2,1,0:T(8,128)S(1)}, f32[3,33,256]{2,1,0:T(8,128)S(1)}, u32[]{:S(2)}, u32[]{:S(2)}) collective-permute-start(f32[3,33,256]{2,1,0:T(8,128)S(1)} %pad_maximum_fusion.3), channel_id=1, source_target_pairs={{0,16},{16,0},{2,18},{18,2},{4,20},{20,4},{6,22},{22,6},{8,24},{24... | collective-permute-start | bytes 304136 | tf_op jit(solution)/shard_map/ppermute | solution.py:18
  56.7 3.0 %collective-permute-start.8 = (f32[3,32,128]{2,1,0:T(8,128)S(1)}, f32[3,32,128]{2,1,0:T(8,128)S(1)}, u32[]{:S(2)}, u32[]{:S(2)}) collective-permute-start(f32[3,32,128]{2,1,0:T(8,128)S(1)} %dynamic-slice_bitcast_fusion), channel_id=1, source_target_pairs={{0,4},{4,0},{2,6},{6,2},{8,12},{12,8},{10,14},{14,10},{16,20},{20,... | collective-permute-start | bytes 147464 | tf_op jit(solution)/shard_map/ppermute | solution.py:18
  59.8 7.5 %collective-permute-start.9 = (f32[3,32,64]{2,1,0:T(8,128)S(1)}, f32[3,32,64]{2,1,0:T(8,128)S(1)}, u32[]{:S(2)}, u32[]{:S(2)}) collective-permute-start(f32[3,32,64]{2,1,0:T(8,128)S(1)} %constant_dynamic-slice_fusion), channel_id=1, source_target_pairs={{0,2},{2,0},{4,6},{6,4},{8,10},{10,8},{12,14},{14,12},{16,18},{18,... | collective-permute-start | bytes 73736 | tf_op jit(solution)/shard_map/ppermute | solution.py:18
where the time goes:
time: 68.9 us; the launch traced here: 68.6 us
  starting transfers between devices  16.5 us (24%)
  waiting for transfers between devices  16.3 us (24%)
  blocking collectives  12.9 us (19%)
  matrix products  9.13 us (13%)
  other arithmetic  6.43 us (9%)
  between operations  5.42 us (8%)
  local copies, waits for them, and re-layouts  1.92 us (3%)
    ppermute x10, starting transfers between devices, from_partner(): return lax.ppermute(block, axis, route)  16.5 us
    ppermute x10, waiting for transfers between devices, from_partner(): return lax.ppermute(block, axis, route)  16.3 us
    all_gather x2, blocking collectives, grid_product(): sources = lax.all_gather(packed, 'tile', axis=2, tiled=True)  12.9 us
    dot_general x2, matrix products, contract(): jnp.einsum('abij,bkj->aki', tensor, vectors, precision=lax.Precision.HIGH...  9.13 us
    another operation x3, other arithmetic, body(): return (displacement, jnp.stack([first_image, second_image]))  1.45 us
    reduce_sum x2, other arithmetic, weights_from(): jnp.sum(samples * jnp.cos(order * angles))  1.4 us
  transfers between devices with their start and end apart: 10, of which 5 were waited for; matrix products, arithmetic and copies ran while one was open for 7% of the time, Pallas kernels for 0%

commit v1 on v0

--- a/solution.py
+++ b/solution.py
@@ -58,7 +58,9 @@
 def grid_product(packed, positions):
     half_bits = (lax.axis_size("blk").bit_length() - 1) // 2
     block_number = lax.axis_index("blk")
-    sources = lax.all_gather(packed, "tile", axis=2, tiled=True)
+    sources = jnp.concatenate(
+        lax.all_to_all(jnp.stack([packed] * lax.axis_size("tile")), "tile", 0, 0), axis=2
+    )
     for bit_number in range(half_bits, 2 * half_bits):
         partner = from_partner(sources, "blk", bit_number)
         sources = jnp.concatenate([sources, partner], axis=2)

time: 68.9 us -> 72.7 us (1.055)
  starting transfers between devices: 16.5 us -> 25.1 us
  blocking collectives: 12.9 us -> 5.26 us
  local copies, waits for them, and re-layouts: 1.92 us -> 3.51 us
  other arithmetic: 6.43 us -> 7.99 us
    all_gather x2 -> x0, blocking collectives: 12.9 us -> none  [grid_product(): sources = lax.all_gather(packed, 'tile', axis=2, tiled=True)]
    all_to_all x0 -> x1, blocking collectives: none -> 5.26 us  [grid_product(): lax.all_to_all(jnp.stack([packed] * lax.axis_size('tile')), 'tile', 0, 0)]
    ppermute x10, starting transfers between devices: 16.5 us -> 21.2 us  [from_partner(): return lax.ppermute(block, axis, route)]
    all_to_all x0 -> x1, starting transfers between devices: none -> 3.95 us  [grid_product(): lax.all_to_all(jnp.stack([packed] * lax.axis_size('tile')), 'tile', 0, 0)]
    all_to_all x0 -> x2, other arithmetic: none -> 1.59 us  [grid_product(): lax.all_to_all(jnp.stack([packed] * lax.axis_size('tile')), 'tile', 0, 0)]
    unnamed x6 -> x14, local copies, waits for them, and re-layouts: 0.02 us -> 1.15 us
    another operation x0 -> x4, other arithmetic: none -> 0.85 us  [grid_product(): jnp.stack([packed] * lax.axis_size('tile'))]
    concatenate x2 -> x0, other arithmetic: 0.82 us -> none  [mobility(): packed = jnp.concatenate([positions[:, None, :], vectors], axis=1)]
  transfers between devices with their start and end apart: 10 -> 11, of which waited for: 5 -> 7; matrix products, arithmetic and copies ran while one was open for 7% -> 7% of each run, Pallas kernels for 0% -> 0%
where the time goes in v1:
time: 72.7 us; the launch traced here: 72.3 us
  starting transfers between devices  25.1 us (35%)
  waiting for transfers between devices  15.9 us (22%)
  matrix products  9.13 us (13%)
  other arithmetic  7.99 us (11%)
  between operations  5.37 us (7%)
  blocking collectives  5.26 us (7%)
  local copies, waits for them, and re-layouts  3.51 us (5%)
    ppermute x10, starting transfers between devices, from_partner(): return lax.ppermute(block, axis, route)  21.2 us
    ppermute x10, waiting for transfers between devices, from_partner(): return lax.ppermute(block, axis, route)  15.9 us
    dot_general x2, matrix products, contract(): jnp.einsum('abij,bkj->aki', tensor, vectors, precision=lax.Precision.HIGH...  9.13 us
    all_to_all x1, blocking collectives, grid_product(): lax.all_to_all(jnp.stack([packed] * lax.axis_size('tile')), 'tile', 0, 0)  5.26 us
    all_to_all x1, starting transfers between devices, grid_product(): lax.all_to_all(jnp.stack([packed] * lax.axis_size('tile')), 'tile', 0, 0)  3.95 us
    all_to_all x2, other arithmetic, grid_product(): lax.all_to_all(jnp.stack([packed] * lax.axis_size('tile')), 'tile', 0, 0)  1.59 us
  transfers between devices with their start and end apart: 11, of which 7 were waited for; matrix products, arithmetic and copies ran while one was open for 7% of the time, Pallas kernels for 0%

profile of v1, /device:TPU:1, one launch (start us, length us, event | category | flops | bytes accessed | tf_op | source)
XLA Modules:
  0.0 72.3 jit_solution(1774940067765653716)
XLA Ops:
  1.4 0.8 %fusion.36 = f32[1,3,33,64]{3,2,1,0:T(8,128)S(1)} fusion(f32[3,1,64]{2,1,0:T(1,128)S(1)} %broadcast_in_dim.2, f32[3,32,64]{2,1,0:T(8,128)} %param.4), kind=kLoop, calls=%fused_computation.53 | loop fusion | flops 6336 | bytes 50688 | tf_op jit(solution)/shard_map/stack | solution.py:62
  3.0 4.0 %all-to-all-start = ((f32[2,1,6336]{2,1,0:T(1,128)}), f32[2,1,6336]{2,1,0:T(1,128)S(1)}, u32[]{:S(2)}, u32[]{:S(2)}) async-start(f32[2,1,6336]{2,1,0:T(1,128)} %reshape.141), calls=%async_computation | async-start | bytes 102400 | tf_op jit(solution)/shard_map/all_to_all | solution.py:62
  6.9 0.8 %maximum_select_fusion.1 = f32[3,128]{1,0:T(4,128)S(1)} fusion(f32[3,64]{1,0:T(4,128)} %param.3, f32[3,64]{1,0:T(4,128)S(1)} %collective-permute-done.2, pred[]{:T(512)S(6)} %eq.29), kind=kLoop, calls=%fused_computation.74 | loop fusion | flops 1152 | bytes 3073 | tf_op jit(solution)/shard_map/jit(_where)/select_n | solution.py:71
  7.8 2.1 %collective-permute-start.3 = (f32[3,128]{1,0:T(4,128)S(1)}, f32[3,128]{1,0:T(4,128)S(1)}, u32[]{:S(2)}, u32[]{:S(2)}) collective-permute-start(f32[3,128]{1,0:T(4,128)S(1)} %maximum_select_fusion.1), channel_id=1, source_target_pairs={{0,4},{4,0},{2,6},{6,2},{8,12},{12,8},{10,14},{14,10},{16,20},{20,... | collective-permute-start | bytes 4616 | tf_op jit(solution)/shard_map/ppermute | solution.py:18
  9.8 1.1 %collective-permute-done.3 = f32[3,128]{1,0:T(4,128)S(1)} collective-permute-done((f32[3,128]{1,0:T(4,128)S(1)}, f32[3,128]{1,0:T(4,128)S(1)}, u32[]{:S(2)}, u32[]{:S(2)}) %collective-permute-start.3) | collective-permute-done | bytes 1568 | tf_op jit(solution)/shard_map/ppermute | solution.py:18
  11.5 0.8 %reduce = f32[2,6336]{1,0:T(2,128)S(1)} reduce(f32[2,1,6336]{2,1,0:T(1,128)S(1)} %all-to-all-done, f32[]{:T(128)} %broadcast.213), dimensions={1}, to_apply=%all_to_all.6.reduce_sub_computation | reduce | bytes 101380 | tf_op jit(solution)/shard_map/all_to_all | solution.py:62
  12.6 1.7 %collective-permute-start = (f32[3,33,128]{2,1,0:T(8,128)S(1)}, f32[3,33,128]{2,1,0:T(8,128)S(1)}, u32[]{:S(2)}, u32[]{:S(2)}) collective-permute-start(f32[3,33,128]{2,1,0:T(8,128)S(1)} %reshape.134), channel_id=1, source_target_pairs={{0,8},{8,0},{2,10},{10,2},{4,12},{12,4},{6,14},{14,6},{16,24},{24,... | collective-permute-start | bytes 152072 | tf_op jit(solution)/shard_map/ppermute | solution.py:18
  14.3 1.6 %collective-permute-done = f32[3,33,128]{2,1,0:T(8,128)S(1)} collective-permute-done((f32[3,33,128]{2,1,0:T(8,128)S(1)}, f32[3,33,128]{2,1,0:T(8,128)S(1)}, u32[]{:S(2)}, u32[]{:S(2)}) %collective-permute-start) | collective-permute-done | bytes 50720 | tf_op jit(solution)/shard_map/ppermute | solution.py:18
  15.9 2.5 %collective-permute-start.1 = (f32[3,33,256]{2,1,0:T(8,128)S(1)}, f32[3,33,256]{2,1,0:T(8,128)S(1)}, u32[]{:S(2)}, u32[]{:S(2)}) collective-permute-start(f32[3,33,256]{2,1,0:T(8,128)S(1)} %pad_maximum_fusion.1), channel_id=1, source_target_pairs={{0,16},{16,0},{2,18},{18,2},{4,20},{20,4},{6,22},{22,6},{8,24},{24... | collective-permute-start | bytes 304136 | tf_op jit(solution)/shard_map/ppermute | solution.py:18
  18.5 4.0 %collective-permute-done.1 = f32[3,33,256]{2,1,0:T(8,128)S(1)} collective-permute-done((f32[3,33,256]{2,1,0:T(8,128)S(1)}, f32[3,33,256]{2,1,0:T(8,128)S(1)}, u32[]{:S(2)}, u32[]{:S(2)}) %collective-permute-start.1) | collective-permute-done | bytes 101408 | tf_op jit(solution)/shard_map/ppermute | solution.py:18
  23.5 4.6 %fusion.16 = f32[32,3,256]{2,0,1:T(8,128)S(1)} fusion(f32[3,256,512]{2,1,0:T(8,128)S(1)} %get-tuple-element.13, f32[3,256,512]{2,1,0:T(8,128)S(1)} %get-tuple-element.12, f32[256,512]{1,0:T(8,128)S(1)} %get-tuple-element.4, f32[3,3]{1,0:T(4,128)S(1)} %fusion.40, f32[3,33,512]{2,1,0:T(8,128)S(1)} %constant_dynamic-update-slice_fusion), kind=kOutput, calls=%fused_computation.20 | convolution fusion | flops 456523776 | bytes 3966976 | tf_op jit(solution)/shard_map/abij,bkj->aki/dot_general | solution.py:40
  28.1 1.4 %collective-permute-start.4 = (f32[3,32,128]{2,1,0:T(8,128)S(1)}, f32[3,32,128]{2,1,0:T(8,128)S(1)}, u32[]{:S(2)}, u32[]{:S(2)}) collective-permute-start(f32[3,32,128]{2,1,0:T(8,128)S(1)} %dynamic-slice_bitcast_fusion.1), channel_id=1, source_target_pairs={{0,4},{4,0},{2,6},{6,2},{8,12},{12,8},{10,14},{14,10},{16,20},{20,... | collective-permute-start | bytes 147464 | tf_op jit(solution)/shard_map/ppermute | solution.py:18
  29.4 1.7 %collective-permute-done.4 = f32[3,32,128]{2,1,0:T(8,128)S(1)} collective-permute-done((f32[3,32,128]{2,1,0:T(8,128)S(1)}, f32[3,32,128]{2,1,0:T(8,128)S(1)}, u32[]{:S(2)}, u32[]{:S(2)}) %collective-permute-start.4) | collective-permute-done | bytes 49184 | tf_op jit(solution)/shard_map/ppermute | solution.py:18
  31.2 4.0 %collective-permute-start.5 = (f32[3,32,64]{2,1,0:T(8,128)S(1)}, f32[3,32,64]{2,1,0:T(8,128)S(1)}, u32[]{:S(2)}, u32[]{:S(2)}) collective-permute-start(f32[3,32,64]{2,1,0:T(8,128)S(1)} %constant_dynamic-slice_fusion.1), channel_id=1, source_target_pairs={{0,2},{2,0},{4,6},{6,4},{8,10},{10,8},{12,14},{14,12},{16,18},{18,... | collective-permute-start | bytes 73736 | tf_op jit(solution)/shard_map/ppermute | solution.py:18
  38.7 5.3 %all_to_all.10 = f32[2,1,6336]{2,1,0:T(1,128)S(1)} all-to-all(f32[2,1,6336]{2,1,0:T(1,128)S(1)} %reshape.143), channel_id=1, replica_groups=mesh['blk'=16,'tile'=2] {'tile'}, dimensions={0} | all-to-all | bytes 101376 | tf_op jit(solution)/shard_map/all_to_all | solution.py:62
  43.9 0.8 %reduce.1 = f32[2,6336]{1,0:T(2,128)S(1)} reduce(f32[2,1,6336]{2,1,0:T(1,128)S(1)} %all_to_all.10, f32[]{:T(128)} %broadcast.213), dimensions={1}, to_apply=%all_to_all.7.reduce_sub_computation | reduce | bytes 101380 | tf_op jit(solution)/shard_map/all_to_all | solution.py:62
  45.0 0.7 %collective-permute-start.6 = (f32[3,33,128]{2,1,0:T(8,128)S(1)}, f32[3,33,128]{2,1,0:T(8,128)S(1)}, u32[]{:S(2)}, u32[]{:S(2)}) collective-permute-start(f32[3,33,128]{2,1,0:T(8,128)S(1)} %reshape.136), channel_id=1, source_target_pairs={{0,8},{8,0},{2,10},{10,2},{4,12},{12,4},{6,14},{14,6},{16,24},{24,... | collective-permute-start | bytes 152072 | tf_op jit(solution)/shard_map/ppermute | solution.py:18
  45.8 2.4 %collective-permute-done.6 = f32[3,33,128]{2,1,0:T(8,128)S(1)} collective-permute-done((f32[3,33,128]{2,1,0:T(8,128)S(1)}, f32[3,33,128]{2,1,0:T(8,128)S(1)}, u32[]{:S(2)}, u32[]{:S(2)}) %collective-permute-start.6) | collective-permute-done | bytes 50720 | tf_op jit(solution)/shard_map/ppermute | solution.py:18
  48.2 2.4 %collective-permute-start.7 = (f32[3,33,256]{2,1,0:T(8,128)S(1)}, f32[3,33,256]{2,1,0:T(8,128)S(1)}, u32[]{:S(2)}, u32[]{:S(2)}) collective-permute-start(f32[3,33,256]{2,1,0:T(8,128)S(1)} %pad_maximum_fusion.3), channel_id=1, source_target_pairs={{0,16},{16,0},{2,18},{18,2},{4,20},{20,4},{6,22},{22,6},{8,24},{24... | collective-permute-start | bytes 304136 | tf_op jit(solution)/shard_map/ppermute | solution.py:18
  50.6 3.6 %collective-permute-done.7 = f32[3,33,256]{2,1,0:T(8,128)S(1)} collective-permute-done((f32[3,33,256]{2,1,0:T(8,128)S(1)}, f32[3,33,256]{2,1,0:T(8,128)S(1)}, u32[]{:S(2)}, u32[]{:S(2)}) %collective-permute-start.7) | collective-permute-done | bytes 101408 | tf_op jit(solution)/shard_map/ppermute | solution.py:18
  55.2 4.6 %fusion.19 = f32[32,3,256]{2,0,1:T(8,128)S(1)} fusion(f32[3,256,512]{2,1,0:T(8,128)S(1)} %get-tuple-element.11, f32[3,256,512]{2,1,0:T(8,128)S(1)} %get-tuple-element.10, f32[256,512]{1,0:T(8,128)S(1)} %get-tuple-element.2, f32[3,3]{1,0:T(4,128)S(1)} %fusion.40, f32[3,33,512]{2,1,0:T(8,128)S(1)} %constant_dynamic-update-slice_fusion.3), kind=kOutput, calls=%fused_computation.21 | convolution fusion | flops 456523776 | bytes 3966976 | tf_op jit(solution)/shard_map/abij,bkj->aki/dot_general | solution.py:40
  59.8 1.6 %collective-permute-start.8 = (f32[3,32,128]{2,1,0:T(8,128)S(1)}, f32[3,32,128]{2,1,0:T(8,128)S(1)}, u32[]{:S(2)}, u32[]{:S(2)}) collective-permute-start(f32[3,32,128]{2,1,0:T(8,128)S(1)} %dynamic-slice_bitcast_fusion), channel_id=1, source_target_pairs={{0,4},{4,0},{2,6},{6,2},{8,12},{12,8},{10,14},{14,10},{16,20},{20,... | collective-permute-start | bytes 147464 | tf_op jit(solution)/shard_map/ppermute | solution.py:18
  61.4 1.5 %collective-permute-done.8 = f32[3,32,128]{2,1,0:T(8,128)S(1)} collective-permute-done((f32[3,32,128]{2,1,0:T(8,128)S(1)}, f32[3,32,128]{2,1,0:T(8,128)S(1)}, u32[]{:S(2)}, u32[]{:S(2)}) %collective-permute-start.8) | collective-permute-done | bytes 49184 | tf_op jit(solution)/shard_map/ppermute | solution.py:18
  62.9 4.6 %collective-permute-start.9 = (f32[3,32,64]{2,1,0:T(8,128)S(1)}, f32[3,32,64]{2,1,0:T(8,128)S(1)}, u32[]{:S(2)}, u32[]{:S(2)}) collective-permute-start(f32[3,32,64]{2,1,0:T(8,128)S(1)} %constant_dynamic-slice_fusion), channel_id=1, source_target_pairs={{0,2},{2,0},{4,6},{6,4},{8,10},{10,8},{12,14},{14,12},{16,18},{18,... | collective-permute-start | bytes 73736 | tf_op jit(solution)/shard_map/ppermute | solution.py:18
  (54 shorter events, 8.4 us)
Async XLA Ops:
  0.6 6.3 %collective-permute-start.2 = (f32[3,64]{1,0:T(4,128)}, f32[3,64]{1,0:T(4,128)S(1)}, u32[]{:S(2)}, u32[]{:S(2)}) collective-permute-start(f32[3,64]{1,0:T(4,128)} %param.3), channel_id=1, source_target_pairs={{0,2},{2,0},{4,6},{6,4},{8,10},{10,8},{12,14},{14,12},{16,18},{18,... | collective-permute-start | bytes 2312 | tf_op jit(solution)/shard_map/ppermute | solution.py:18
  3.0 8.0 %all-to-all-start = ((f32[2,1,6336]{2,1,0:T(1,128)}), f32[2,1,6336]{2,1,0:T(1,128)S(1)}, u32[]{:S(2)}, u32[]{:S(2)}) async-start(f32[2,1,6336]{2,1,0:T(1,128)} %reshape.141), calls=%async_computation | async-start | bytes 102400 | tf_op jit(solution)/shard_map/all_to_all | solution.py:62
  7.8 3.2 %collective-permute-start.3 = (f32[3,128]{1,0:T(4,128)S(1)}, f32[3,128]{1,0:T(4,128)S(1)}, u32[]{:S(2)}, u32[]{:S(2)}) collective-permute-start(f32[3,128]{1,0:T(4,128)S(1)} %maximum_select_fusion.1), channel_id=1, source_target_pairs={{0,4},{4,0},{2,6},{6,2},{8,12},{12,8},{10,14},{14,10},{16,20},{20,... | collective-permute-start | bytes 4616 | tf_op jit(solution)/shard_map/ppermute | solution.py:18
  12.6 3.4 %collective-permute-start = (f32[3,33,128]{2,1,0:T(8,128)S(1)}, f32[3,33,128]{2,1,0:T(8,128)S(1)}, u32[]{:S(2)}, u32[]{:S(2)}) collective-permute-start(f32[3,33,128]{2,1,0:T(8,128)S(1)} %reshape.134), channel_id=1, source_target_pairs={{0,8},{8,0},{2,10},{10,2},{4,12},{12,4},{6,14},{14,6},{16,24},{24,... | collective-permute-start | bytes 152072 | tf_op jit(solution)/shard_map/ppermute | solution.py:18
  15.9 6.6 %collective-permute-start.1 = (f32[3,33,256]{2,1,0:T(8,128)S(1)}, f32[3,33,256]{2,1,0:T(8,128)S(1)}, u32[]{:S(2)}, u32[]{:S(2)}) collective-permute-start(f32[3,33,256]{2,1,0:T(8,128)S(1)} %pad_maximum_fusion.1), channel_id=1, source_target_pairs={{0,16},{16,0},{2,18},{18,2},{4,20},{20,4},{6,22},{22,6},{8,24},{24... | collective-permute-start | bytes 304136 | tf_op jit(solution)/shard_map/ppermute | solution.py:18
  23.5 11.8 %copy-start.1 = (f32[2]{0:T(128)S(1)}, f32[2]{0:T(128)}, u32[]{:S(2)}) copy-start(f32[2]{0:T(128)} %param.5) | copy-start | bytes 28
  23.5 14.9 %copy-start = (f32[3,32,64]{2,1,0:T(8,128)S(1)}, f32[3,32,64]{2,1,0:T(8,128)}, u32[]{:S(2)}) copy-start(f32[3,32,64]{2,1,0:T(8,128)} %param.4) | copy-start | bytes 73732
  28.1 3.0 %collective-permute-start.4 = (f32[3,32,128]{2,1,0:T(8,128)S(1)}, f32[3,32,128]{2,1,0:T(8,128)S(1)}, u32[]{:S(2)}, u32[]{:S(2)}) collective-permute-start(f32[3,32,128]{2,1,0:T(8,128)S(1)} %dynamic-slice_bitcast_fusion.1), channel_id=1, source_target_pairs={{0,4},{4,0},{2,6},{6,2},{8,12},{12,8},{10,14},{14,10},{16,20},{20,... | collective-permute-start | bytes 147464 | tf_op jit(solution)/shard_map/ppermute | solution.py:18
  31.2 7.2 %collective-permute-start.5 = (f32[3,32,64]{2,1,0:T(8,128)S(1)}, f32[3,32,64]{2,1,0:T(8,128)S(1)}, u32[]{:S(2)}, u32[]{:S(2)}) collective-permute-start(f32[3,32,64]{2,1,0:T(8,128)S(1)} %constant_dynamic-slice_fusion.1), channel_id=1, source_target_pairs={{0,2},{2,0},{4,6},{6,4},{8,10},{10,8},{12,14},{14,12},{16,18},{18,... | collective-permute-start | bytes 73736 | tf_op jit(solution)/shard_map/ppermute | solution.py:18
  45.0 3.1 %collective-permute-start.6 = (f32[3,33,128]{2,1,0:T(8,128)S(1)}, f32[3,33,128]{2,1,0:T(8,128)S(1)}, u32[]{:S(2)}, u32[]{:S(2)}) collective-permute-start(f32[3,33,128]{2,1,0:T(8,128)S(1)} %reshape.136), channel_id=1, source_target_pairs={{0,8},{8,0},{2,10},{10,2},{4,12},{12,4},{6,14},{14,6},{16,24},{24,... | collective-permute-start | bytes 152072 | tf_op jit(solution)/shard_map/ppermute | solution.py:18
  48.2 6.0 %collective-permute-start.7 = (f32[3,33,256]{2,1,0:T(8,128)S(1)}, f32[3,33,256]{2,1,0:T(8,128)S(1)}, u32[]{:S(2)}, u32[]{:S(2)}) collective-permute-start(f32[3,33,256]{2,1,0:T(8,128)S(1)} %pad_maximum_fusion.3), channel_id=1, source_target_pairs={{0,16},{16,0},{2,18},{18,2},{4,20},{20,4},{6,22},{22,6},{8,24},{24... | collective-permute-start | bytes 304136 | tf_op jit(solution)/shard_map/ppermute | solution.py:18
  59.8 3.1 %collective-permute-start.8 = (f32[3,32,128]{2,1,0:T(8,128)S(1)}, f32[3,32,128]{2,1,0:T(8,128)S(1)}, u32[]{:S(2)}, u32[]{:S(2)}) collective-permute-start(f32[3,32,128]{2,1,0:T(8,128)S(1)} %dynamic-slice_bitcast_fusion), channel_id=1, source_target_pairs={{0,4},{4,0},{2,6},{6,2},{8,12},{12,8},{10,14},{14,10},{16,20},{20,... | collective-permute-start | bytes 147464 | tf_op jit(solution)/shard_map/ppermute | solution.py:18
  62.9 8.0 %collective-permute-start.9 = (f32[3,32,64]{2,1,0:T(8,128)S(1)}, f32[3,32,64]{2,1,0:T(8,128)S(1)}, u32[]{:S(2)}, u32[]{:S(2)}) collective-permute-start(f32[3,32,64]{2,1,0:T(8,128)S(1)} %constant_dynamic-slice_fusion), channel_id=1, source_target_pairs={{0,2},{2,0},{4,6},{6,4},{8,10},{10,8},{12,14},{14,12},{16,18},{18,... | collective-permute-start | bytes 73736 | tf_op jit(solution)/shard_map/ppermute | solution.py:18
